TPU v7x, 512 devices: a 8x2x16 block of a 8x8x16 slice. The times are simulated.
512 devices in a mesh: frag: 2 (over y), band: 128 (over z, x), slab: 2 (over core).
Axes of the slice: x: 8, y: 2, z: 16, core: 2. Of those that a mesh axis runs over, the one named last changes fastest.
The devices are a block of a 8x8x16 slice.
Arguments:
- wavefunctions: bfloat16 [2048, 16384], P('band', ('frag', 'slab')), parts along dimension 1, may hold values from -6 to 6
- eigvec: bfloat16 [2048, 4096], P(None, ('frag', 'band', 'slab')), parts along dimension 1, may hold values from -1 to 1, as said below
- occupation: float32 [4096], P('frag'), parts along dimension 0, may hold values from 0.1 to 2
Outputs:
- rotated: float32 [2048, 16384], P('band', ('frag', 'slab')), parts along dimension 1
- density: float32 [16384], P(('frag', 'slab')), parts along dimension 0
There are 2 independent parts, one for each index of `frag`. A program takes and returns all parts, laid end to end along the dimension named above; each array names one. Nothing has to cross between parts.
Inputs may be any that keep to these rules, and one draw needn't show every extreme that they name: eigvec is an orthogonal matrix rounded to bfloat16.
All inputs are finite; a program needn't handle non-finite values.
Results may differ from a plain program's by a relative error of at most 0.0003.
Values may be sent and summed in bfloat16 or wider, within the bound.
No kernel may reach another device: no remote copies, remote signals or barrier semaphores. Data moves between devices by JAX's collectives and lax.ppermute only.
A program may use at most 64 MiB of HBM per device.

v0:
```python
import jax
import jax.numpy as jnp
from jax import lax
from jax.sharding import Mesh
from jax.sharding import PartitionSpec as P

BAND = ("band_0", "band_1")
BAND_SLAB = ("band_0", "band_1", "slab")
FRAG_BAND_SLAB = ("frag", "band_0", "band_1", "slab")


def in_blocks(array, dim, peers):
    dims = array.shape
    blocks = array.reshape(*dims[:dim], peers, dims[dim] // peers, *dims[dim + 1 :])
    return jnp.moveaxis(blocks, dim, 0)


def laid_out(blocks, dim):
    blocks = jnp.moveaxis(blocks, 0, dim)
    dims = blocks.shape
    return blocks.reshape(*dims[:dim], dims[dim] * dims[dim + 1], *dims[dim + 2 :])


def exchange_in_order(blocks, axes, turns):
    inside = blocks.shape[1:]
    result = blocks.reshape(*(lax.axis_size(a) for a in axes), *inside)
    for k in turns:
        result = lax.all_to_all(result, axes[k], k, k, tiled=True)
    return result.reshape(-1, *inside)


def one_axis_at_a_time(array, axes, turns, split_dim, concat_dim):
    blocks = in_blocks(array, split_dim, lax.axis_size(axes))
    return laid_out(exchange_in_order(blocks, axes, turns), concat_dim)


def stacked_from(array, axes, turns):
    blocks = array
    for k in turns:
        blocks = lax.all_gather(blocks, axes[k])
    done = turns[::-1]
    back = [done.index(k) for k in range(len(axes))]
    blocks = blocks.transpose(*back, *range(len(axes), blocks.ndim))
    return blocks.reshape(-1, *array.shape)


def whole_of(array, axes, turns, dim):
    return laid_out(stacked_from(array, axes, turns), dim)


def local(wavefunctions, eigvec, occupation):
    total_bands = eigvec.shape[0]
    by_points = one_axis_at_a_time(wavefunctions, BAND, (0, 1), 1, 0)
    point_rows = lax.dot_general(
        lax.all_gather(eigvec, BAND_SLAB, axis=1, tiled=True),
        by_points,
        (((0,), (0,)), ((), ())),
        preferred_element_type=jnp.float32,
    )
    rotated = lax.all_to_all(point_rows, BAND, split_axis=0, concat_axis=1, tiled=True)
    local_density = jnp.dot(
        occupation,
        point_rows * point_rows,
        precision=lax.Precision.HIGHEST,
        preferred_element_type=jnp.float32,
    ) / jnp.float32(total_bands)
    density = whole_of(local_density, BAND, (0, 1), 0)
    return (rotated, density)


def solution(mesh):
    torus = Mesh(
        mesh.devices.reshape(mesh.shape["frag"], 16, 8, mesh.shape["slab"]),
        ("frag", "band_0", "band_1", "slab"),
    )
    in_specs = (P(BAND, ("frag", "slab")), P(None, FRAG_BAND_SLAB), P("frag"))
    out_specs = (P(BAND, ("frag", "slab")), P(("frag", "slab")))
    return jax.shard_map(local, mesh=torus, in_specs=in_specs, out_specs=out_specs, check_vma=False)
```

profile of v0, /device:TPU:68, one launch (start us, length us, event | category | flops | bytes accessed | tf_op | source)
XLA Modules:
  0.0 287.4 jit_solution(17181273735163144986)
XLA Ops:
  7.3 0.7 all-gather.4.cloned.1.call-update
  8.0 1.3 reshape.13
  9.3 0.3 copy.18
  9.6 0.5 reshape.24
  10.2 58.1 %all_to_all.29 = bf16[16,2,2048]{2,1,0:T(2,128)(2,1)S(1)} all-to-all(bf16[16,2,2048]{2,1,0:T(2,128)(2,1)S(1)} %reshape.24), channel_id=1, replica_groups=mesh['frag'=2,'band_0'=16,'band_1'=8,'slab'=2] {'band_0'}, dimensions={0} | all-to-all | bytes 262144 | tf_op jit(solution)/shard_map/all_to_all | solution.py:28
  68.3 0.3 reshape.25
  68.6 0.5 reshape.26
  69.1 14.0 %all_to_all.30 = bf16[8,2,4096]{2,1,0:T(2,128)(2,1)S(1)} all-to-all(bf16[8,2,4096]{2,1,0:T(2,128)(2,1)S(1)} %reshape.26), channel_id=1, replica_groups=mesh['frag'=2,'band_0'=16,'band_1'=8,'slab'=2] {'band_1'}, dimensions={0} | all-to-all | bytes 262144 | tf_op jit(solution)/shard_map/all_to_all | solution.py:28
  83.1 0.3 reshape.27
  83.4 108.6 %all-gather.4.cloned.1.call-done = bf16[2048,2048]{0,1:T(8,128)(2,1)} async-done(((bf16[2048,8]{0,1:T(8,128)(2,1)}), bf16[2048,2048]{0,1:T(8,128)(2,1)}) %all-gather.4.cloned.1.call-update) | async-done | bytes 8388624 | tf_op jit(solution)/shard_map/all_gather | solution.py:55
  192.0 5.9 %fusion.2 = f32[2048,32]{0,1:T(8,128)S(1)} fusion(bf16[2048,2048]{0,1:T(8,128)(2,1)} %all-gather.4.cloned.1.call-done, bf16[2048,32]{1,0:T(8,128)(2,1)S(1)} %bitcast.25), kind=kOutput, calls=%fused_computation.4 | convolution fusion | flops 268435456 | bytes 8781824 | tf_op jit(solution)/shard_map/dot_general | solution.py:54
  197.9 0.3 copy.21
  198.3 1.2 reshape.28
  199.5 15.7 %all-to-all-start.2 = ((f32[128,1,512]{2,1,0:T(1,128)}), f32[128,1,512]{2,1,0:T(1,128)S(1)}, u32[]{:S(2)}, u32[]{:S(2)}) async-start(f32[128,1,512]{2,1,0:T(1,128)} %reshape.28), calls=%async_computation.2 | async-start | bytes 524288 | tf_op jit(solution)/shard_map/all_to_all | solution.py:60
  215.2 1.3 dynamic-slice
  217.1 0.3 fusion
  217.6 32.8 %all-reduce = f32[512]{0:T(512)S(1)} all-reduce(f32[512]{0:T(512)S(1)} %dynamic-update-slice), channel_id=2, replica_groups=mesh['frag'=2,'band_0'=16,'band_1'=8,'slab'=2] {'band_0'}, use_global_device_ids=true, to_apply=%add | all-reduce | flops 512 | bytes 4096
  250.5 25.8 %all-gather.1 = f32[128,32]{1,0:T(8,128)S(1)} all-gather(f32[16,32]{1,0:T(8,128)S(1)} %reshape.15), channel_id=3, replica_groups=mesh['frag'=2,'band_0'=16,'band_1'=8,'slab'=2] {'band_1'}, dimensions={0}, use_global_device_ids=true | all-gather | bytes 18432 | tf_op jit(solution)/shard_map/all_gather | solution.py:40
  276.3 0.7 reshape_reshape.7
  277.0 0.5 broadcast.2
  277.5 1.3 reduce
  278.8 0.3 reshape.29
  279.0 0.3 copy.22
  279.4 1.2 all_to_all.25
  (10 shorter events, 0.5 us)
Async XLA Ops:
  7.2 209.9 %copy-start = (f32[2048]{0:T(1024)S(1)}, f32[2048]{0:T(1024)}, u32[]{:S(2)}) copy-start(f32[2048]{0:T(1024)} %param.5) | copy-start | bytes 24580
  7.2 184.8 %all-gather.4.cloned.1.call-start = ((), (), s32[]{:S(2)}) async-start(), calls=%async_computation.3 | async-start | bytes 8421376 | tf_op jit(solution)/shard_map/all_gather | solution.py:55
  199.5 77.5 %all-to-all-start.2 = ((f32[128,1,512]{2,1,0:T(1,128)}), f32[128,1,512]{2,1,0:T(1,128)S(1)}, u32[]{:S(2)}, u32[]{:S(2)}) async-start(f32[128,1,512]{2,1,0:T(1,128)} %reshape.28), calls=%async_computation.2 | async-start | bytes 524288 | tf_op jit(solution)/shard_map/all_to_all | solution.py:60
Sparse Core Ops, SparseCore 0:
  11.2 180.7 all-gather.3
where the time goes:
time: 288 us; the launch traced here: 287 us
  blocking collectives  131 us (45%)
  waiting for transfers between devices  109 us (38%)
  starting transfers between devices  15.8 us (5%)
  between operations  14.8 us (5%)
  local copies, waits for them, and re-layouts  9.42 us (3%)
  matrix products  6.21 us (2%)
    all_gather x1, waiting for transfers between devices, local(): lax.all_gather(eigvec, BAND_SLAB, axis=1, tiled=True)  109 us
    all_to_all x2, blocking collectives, exchange_in_order(): result = lax.all_to_all(result, axes[k], k, k, tiled=True)  72.1 us
    unnamed x1, blocking collectives  32.8 us
    all_gather x1, blocking collectives, stacked_from(): blocks = lax.all_gather(blocks, axes[k])  25.8 us
    all_to_all x1, starting transfers between devices, local(): lax.all_to_all(point_rows, BAND, split_axis=0, concat_axis=1, tiled=True)  15.7 us
    dot_general x1, matrix products, local(): lax.dot_general(lax.all_gather(eigvec, BAND_SLAB, axis=1, tiled=True), by...  5.94 us
  transfers between devices with their start and end apart: 2, of which 1 were waited for; matrix products, arithmetic and copies ran while one was open for 2% of the time, Pallas kernels for 0%

commit v1 on v0

--- a/solution.py
+++ b/solution.py
@@ -52,7 +52,9 @@
     total_bands = eigvec.shape[0]
     by_points = one_axis_at_a_time(wavefunctions, BAND, (0, 1), 1, 0)
     point_rows = lax.dot_general(
-        lax.all_gather(eigvec, BAND_SLAB, axis=1, tiled=True),
+        jnp.concatenate(
+            lax.all_to_all(jnp.stack([eigvec] * lax.axis_size(BAND_SLAB)), BAND_SLAB, 0, 0), axis=1
+        ),
         by_points,
         (((0,), (0,)), ((), ())),
         preferred_element_type=jnp.float32,

time: 288 us -> 547 us (1.90)
  the two profiles are of different devices: /device:TPU:68 before, /device:TPU:80 now
where the time goes in v1:
time: 547 us; the launch traced here: 546 us
  waiting for transfers between devices  359 us (66%)
  blocking collectives  130 us (24%)
  starting transfers between devices  33.8 us (6%)
  local copies, waits for them, and re-layouts  14.5 us (3%)
  matrix products  6.21 us (1%)
    all_to_all x1, waiting for transfers between devices, local(): lax.all_to_all(jnp.stack([eigvec] * lax.axis_size(BAND_SLAB)), BAND_SLAB,...  359 us
    all_to_all x2, blocking collectives, exchange_in_order(): result = lax.all_to_all(result, axes[k], k, k, tiled=True)  74.3 us
    unnamed x1, blocking collectives  30.4 us
    all_gather x1, blocking collectives, stacked_from(): blocks = lax.all_gather(blocks, axes[k])  25.6 us
    all_to_all x1, starting transfers between devices, local(): lax.all_to_all(jnp.stack([eigvec] * lax.axis_size(BAND_SLAB)), BAND_SLAB,...  17.7 us
    all_to_all x1, starting transfers between devices, local(): lax.all_to_all(point_rows, BAND, split_axis=0, concat_axis=1, tiled=True)  16.1 us
  transfers between devices with their start and end apart: 2, of which 1 were waited for; matrix products, arithmetic and copies ran while one was open for 1% of the time, Pallas kernels for 0%

profile of v1, /device:TPU:80, one launch (start us, length us, event | category | flops | bytes accessed | tf_op | source)
XLA Modules:
  0.0 546.4 jit_solution(7760398969740612055)
XLA Ops:
  0.6 1.3 reshape.23
  2.0 0.3 copy.19
  2.3 0.5 reshape.34
  2.8 58.1 %all_to_all.34 = bf16[16,2,2048]{2,1,0:T(2,128)(2,1)S(1)} all-to-all(bf16[16,2,2048]{2,1,0:T(2,128)(2,1)S(1)} %reshape.34), channel_id=1, replica_groups=mesh['frag'=2,'band_0'=16,'band_1'=8,'slab'=2] {'band_0'}, dimensions={0} | all-to-all | bytes 262144 | tf_op jit(solution)/shard_map/all_to_all | solution.py:28
  60.9 0.3 reshape.35
  61.2 0.5 reshape.36
  61.8 16.2 %all_to_all.35 = bf16[8,2,4096]{2,1,0:T(2,128)(2,1)S(1)} all-to-all(bf16[8,2,4096]{2,1,0:T(2,128)(2,1)S(1)} %reshape.36), channel_id=1, replica_groups=mesh['frag'=2,'band_0'=16,'band_1'=8,'slab'=2] {'band_1'}, dimensions={0} | all-to-all | bytes 262144 | tf_op jit(solution)/shard_map/all_to_all | solution.py:28
  78.0 5.0 stack.2
  83.0 17.7 %all-to-all-start = ((bf16[256,2048,8]{1,2,0:T(8,128)(2,1)}), bf16[256,2048,8]{1,2,0:T(8,128)(2,1)}, u32[]{:S(2)}, u32[]{:S(2)}) async-start(bf16[256,2048,8]{1,2,0:T(8,128)(2,1)} %stack.2), calls=%async_computation | async-start | bytes 16777216 | tf_op jit(solution)/shard_map/all_to_all | solution.py:56
  101.0 358.9 %all-to-all-done = bf16[256,2048,8]{1,2,0:T(8,128)(2,1)} async-done(((bf16[256,2048,8]{1,2,0:T(8,128)(2,1)}), bf16[256,2048,8]{1,2,0:T(8,128)(2,1)}, u32[]{:S(2)}, u32[]{:S(2)}) %all-to-all-start) | async-done | bytes 8388640 | tf_op jit(solution)/shard_map/all_to_all | solution.py:56
  459.9 5.9 %fusion = f32[2048,32]{0,1:T(8,128)S(1)} fusion(bf16[2048,32]{1,0:T(8,128)(2,1)S(1)} %bitcast.29, bf16[256,2048,8]{1,2,0:T(8,128)(2,1)} %all-to-all-done), kind=kOutput, calls=%fused_computation | convolution fusion | flops 268435456 | bytes 8781824 | tf_op jit(solution)/shard_map/dot_general | solution.py:54
  465.9 0.3 copy.22
  466.2 1.2 reshape.38
  467.4 16.1 %all-to-all-start.3 = ((f32[128,1,512]{2,1,0:T(1,128)}), f32[128,1,512]{2,1,0:T(1,128)S(1)}, u32[]{:S(2)}, u32[]{:S(2)}) async-start(f32[128,1,512]{2,1,0:T(1,128)} %reshape.38), calls=%async_computation.3 | async-start | bytes 524288 | tf_op jit(solution)/shard_map/all_to_all | solution.py:62
  483.5 1.3 dynamic-slice
  485.4 0.3 fusion.2
  485.9 30.4 %all-reduce = f32[512]{0:T(512)S(1)} all-reduce(f32[512]{0:T(512)S(1)} %dynamic-update-slice), channel_id=2, replica_groups=mesh['frag'=2,'band_0'=16,'band_1'=8,'slab'=2] {'band_0'}, use_global_device_ids=true, to_apply=%add | all-reduce | flops 512 | bytes 4096
  516.4 25.6 %all-gather.1 = f32[128,32]{1,0:T(8,128)S(1)} all-gather(f32[16,32]{1,0:T(8,128)S(1)} %reshape.25), channel_id=3, replica_groups=mesh['frag'=2,'band_0'=16,'band_1'=8,'slab'=2] {'band_1'}, dimensions={0}, use_global_device_ids=true | all-gather | bytes 18432 | tf_op jit(solution)/shard_map/all_gather | solution.py:40
  542.1 0.7 reshape_reshape.7
  542.7 0.5 broadcast.4
  543.3 1.3 reduce
  544.5 0.3 reshape.39
  544.8 0.3 copy.23
  545.2 1.2 all_to_all.29
  (10 shorter events, 0.7 us)
Async XLA Ops:
  0.6 484.8 %copy-start = (f32[2048]{0:T(1024)S(1)}, f32[2048]{0:T(1024)}, u32[]{:S(2)}) copy-start(f32[2048]{0:T(1024)} %param.5) | copy-start | bytes 24580
  83.0 377.0 %all-to-all-start = ((bf16[256,2048,8]{1,2,0:T(8,128)(2,1)}), bf16[256,2048,8]{1,2,0:T(8,128)(2,1)}, u32[]{:S(2)}, u32[]{:S(2)}) async-start(bf16[256,2048,8]{1,2,0:T(8,128)(2,1)} %stack.2), calls=%async_computation | async-start | bytes 16777216 | tf_op jit(solution)/shard_map/all_to_all | solution.py:56
  467.4 75.3 %all-to-all-start.3 = ((f32[128,1,512]{2,1,0:T(1,128)}), f32[128,1,512]{2,1,0:T(1,128)S(1)}, u32[]{:S(2)}, u32[]{:S(2)}) async-start(f32[128,1,512]{2,1,0:T(1,128)} %reshape.38), calls=%async_computation.3 | async-start | bytes 524288 | tf_op jit(solution)/shard_map/all_to_all | solution.py:62
